TPU v7x, 128 devices: a whole 4x4x4 slice. The times are simulated.
128 devices in a mesh: view: 4 (over z_hi, core), depth: 32 (over z_lo, y, x).
Axes of the slice: x: 4, y: 4, z: 4 (z_hi: 2, z_lo: 2; z = z_hi * 2 + z_lo), core: 2. Of those that a mesh axis runs over, the one named last changes fastest.
Arguments:
- volume: float32 [512, 128, 2048], P(('view', 'depth')), may hold values from -6 to 6
- step_weights: float32 [4, 8, 64], P('view'), may hold values from -0.75 to 0.75
- row_interp: float32 [4, 64, 64], P('view'), may hold values from -0.75 to 0.75
- col_interp: float32 [4, 64, 64], P('view'), may hold values from -0.75 to 0.75
- tf_table: float32 [8, 8], replicated, may hold values from -3 to 3
- materials: int32 [8, 2, 32], P(None, None, 'depth'), may hold values from 0 to 7
- entry: int32 [4, 512, 128], P('view'), may hold values from 0 to 15
Outputs:
- picture: float32 [4, 3, 512, 128], P('view', None, 'depth')
All inputs are finite; a program needn't handle non-finite values.
Results may differ from a plain program's by a relative error of at most 0.00018.
Values sent between devices are 32-bit elements; how exact they have to be, the bound alone decides.
A program may use at most 64 MiB of HBM per device.

v0:
```python
import jax
import jax.numpy as jnp
from jax import lax
from jax.sharding import Mesh
from jax.sharding import PartitionSpec as P

DEPTH = ("depth_0", "depth_1", "depth_2")
VIEW_DEPTH = ("view", "depth_0", "depth_1", "depth_2")


def nothing_yet(shard, identity):
    return jnp.broadcast_to(jnp.asarray(identity, shard.dtype), shard.shape)


def carried_in(shard, axes, combine, identity):
    before = start = nothing_yet(shard, identity)
    total = shard
    for axis in reversed(axes):
        peers, index = (lax.axis_size(axis), lax.axis_index(axis))
        pieces = lax.all_gather(total, axis)
        inside, total = (start, start)
        for k in range(peers):
            passed = k < index
            total = combine(total, pieces[k])
            inside = jnp.where(passed, total, inside)
        before = combine(inside, before)
    return before


def in_blocks(shard, dim, peers):
    dims = shard.shape
    blocks = shard.reshape(*dims[:dim], peers, dims[dim] // peers, *dims[dim + 1 :])
    return jnp.moveaxis(blocks, dim, 0)


def summed_on_arrival(shard, axis, dim):
    peers = lax.axis_size(axis)
    blocks = lax.all_to_all(in_blocks(shard, dim, peers), axis, 0, 0, tiled=True)
    return jnp.sum(blocks, axis=0)


def finish_brick(first, rows_map, cols_map):
    highest = lax.Precision.HIGHEST
    edge = rows_map.shape[0]
    count_steps, total_rows, total_cols = first.shape
    second = first.reshape(count_steps, total_rows // edge, edge, total_cols)
    second = jnp.einsum("stky,rk->stry", second, rows_map, precision=highest)
    third = second.reshape(count_steps, total_rows, total_cols // edge, edge)
    third = jnp.einsum("szuj,cj->szuc", third, cols_map, precision=highest)
    return third.reshape(count_steps, total_rows, total_cols)


def expand_classes(classes, tf_table, edge):
    choices_range = jnp.arange(tf_table.shape[0], dtype=jnp.int32)
    onehot = (classes[:, :, None] == choices_range).astype(jnp.float32)
    tiles = jnp.einsum("abm,mc->cab", onehot, tf_table, precision=lax.Precision.HIGHEST)
    count_coef, tiles_rows, tiles_cols = tiles.shape
    spread = jnp.broadcast_to(
        tiles[:, :, None, :, None], (count_coef, tiles_rows, edge, tiles_cols, edge)
    )
    return spread.reshape(count_coef, tiles_rows * edge, tiles_cols * edge)


def shade(samples, coefficients, live_mask, step_length):
    emission = jax.nn.softplus(coefficients[0:3, None] * samples[None] + coefficients[3:6, None])
    tau = (
        step_length
        * live_mask[None]
        * jax.nn.softplus(coefficients[6][None] * samples + coefficients[7][None])
    )
    earlier = jnp.cumsum(tau, axis=0) - tau
    weights = jnp.exp(-earlier) * (1.0 - jnp.exp(-tau))
    colours = jnp.sum(weights[None] * emission, axis=1)
    passed = jnp.exp(-jnp.sum(tau, axis=0))
    return (colours, passed)


def multiply(earlier, later):
    return earlier * later


def shards(volume, step_weights, row_interp, col_interp, tf_table, materials, entry):
    view_count = lax.axis_size("view")
    depth_count = lax.axis_size(DEPTH)
    depth_index = lax.axis_index(DEPTH)
    planes, lateral, span_cells = volume.shape
    brick_edge = span_cells // depth_count
    all_weights = lax.all_gather(step_weights, "view", axis=0, tiled=True)
    count_steps = all_weights.shape[1]
    cells = volume.reshape(planes, lateral, depth_count, brick_edge)
    contracted = jnp.einsum("zybi,gsi->gbszy", cells, all_weights, precision=lax.Precision.HIGHEST)
    contracted = contracted.reshape(view_count * depth_count, count_steps, planes, lateral)
    received = lax.all_to_all(contracted, VIEW_DEPTH, split_axis=0, concat_axis=2, tiled=True)
    samples = finish_brick(received[0], row_interp[0], col_interp[0])
    coefficients = expand_classes(materials[:, :, 0], tf_table, brick_edge)
    live_mask = (entry[0] <= depth_index).astype(jnp.float32)
    step_length = 2.0 / (samples.shape[0] * depth_count)
    colours, passed = shade(samples, coefficients, live_mask, step_length)
    before = carried_in(passed, DEPTH, multiply, jnp.ones_like(passed))
    terms = before[None] * colours
    rows_part = summed_on_arrival(terms, DEPTH, 1)
    return rows_part[None]


def solution(mesh):
    torus = Mesh(
        mesh.devices.reshape(mesh.shape["view"], 2, 4, 4), ("view", "depth_0", "depth_1", "depth_2")
    )
    return jax.shard_map(
        shards,
        mesh=torus,
        in_specs=(
            P(VIEW_DEPTH, None, None),
            P("view", None, None),
            P("view", None, None),
            P("view", None, None),
            P(),
            P(None, None, DEPTH),
            P("view", None, None),
        ),
        out_specs=P("view", None, DEPTH, None),
        check_vma=False,
    )
```

profile of v0, /device:TPU:0, one launch (start us, length us, event | category | flops | bytes accessed | tf_op | source)
XLA Modules:
  0.0 162.9 jit_solution(9018118237173368795)
XLA Ops:
  6.5 5.4 %copy.64 = f32[4,128,2048]{1,2,0:T(8,128)} copy(f32[4,128,2048]{2,1,0:T(8,128)} %param.7) | data formatting | bytes 8388608 | tf_op args[0]
  11.9 7.2 %all_gather.15 = f32[4,8,64]{2,1,0:T(8,128)S(1)} all-gather(f32[1,8,64]{2,1,0:T(8,128)S(1)} %copy-done.6), channel_id=1, replica_groups=mesh['view'=4,'depth_0'=2,'depth_1'=4,'depth_2'=4] {'view'}, dimensions={0}, use_global_device_ids=true | all-gather | bytes 10240 | tf_op jit(solution)/shard_map/all_gather | solution.py:88
  19.1 3.9 %convolution_bitcast_fusion.1 = f32[4,32,8,4,128]{4,2,1,3,0:T(8,128)S(1)} fusion(f32[4,128,32,64,1]{1,3,2,0,4:T(8,128)} %bitcast.69, f32[4,8,64]{2,1,0:T(8,128)S(1)} %all_gather.15), kind=kOutput, calls=%fused_computation.13 | convolution fusion | flops 402653184 | bytes 6299648 | tf_op jit(solution)/shard_map/zybi,gsi->gbszy/dot_general | solution.py:91
  23.0 1.6 %copy.65 = f32[4,32,8,4,128]{4,2,3,1,0:T(8,128)} copy(f32[4,32,8,4,128]{4,2,1,3,0:T(8,128)S(1)} %convolution_bitcast_fusion.1) | data formatting | bytes 4194304 | tf_op jit(solution)/shard_map/zybi,gsi->gbszy/transpose | solution.py:91
  24.6 10.6 %all-to-all-start = ((f32[128,8,4,128]{3,1,2,0:T(8,128)}), f32[128,8,4,128]{3,1,2,0:T(8,128)S(1)}, u32[]{:S(2)}, u32[]{:S(2)}) async-start(f32[128,8,4,128]{3,1,2,0:T(8,128)} %bitcast.71), calls=%async_computation | async-start | bytes 4194304 | tf_op jit(solution)/shard_map/all_to_all | solution.py:93
  36.3 28.8 %all-to-all-done = f32[128,8,4,128]{3,1,2,0:T(8,128)S(1)} async-done(((f32[128,8,4,128]{3,1,2,0:T(8,128)}), f32[128,8,4,128]{3,1,2,0:T(8,128)S(1)}, u32[]{:S(2)}, u32[]{:S(2)}) %all-to-all-start) | async-done | bytes 2097184 | tf_op jit(solution)/shard_map/all_to_all | solution.py:93
  65.8 2.0 %convolution_bitcast_fusion = f32[8,8,64,128]{3,2,1,0:T(8,128)S(1)} fusion(f32[8,8,64,128]{3,2,1,0:T(8,128)S(1)} %bitcast.72, f32[1,64,64]{2,1,0:T(8,128)S(1)} %copy-done.5), kind=kOutput, calls=%fused_computation.12 | convolution fusion | flops 402653184 | bytes 4210688 | tf_op jit(solution)/shard_map/stky,rk->stry/dot_general | solution.py:47
  67.8 3.7 %reshape.111 = f32[8,512,2,64]{3,2,1,0:T(2,128)} reshape(f32[8,8,64,128]{3,2,1,0:T(8,128)S(1)} %convolution_bitcast_fusion) | data formatting | bytes 4194304 | tf_op jit(solution)/shard_map/reshape | solution.py:48
  71.5 7.0 %fusion.10 = (u8[512,2,64]{0,2,1:T(8,128)(4,1)S(1)}, f32[8,512,2,64]{1,3,2,0:T(8,128)S(1)}) fusion(f32[512,2]{0,1:T(2,128)S(1)} %broadcast_in_dim.39, f32[512,2]{0,1:T(2,128)S(1)} %broadcast_in_dim.37, f32[1,64,64]{2,1,0:T(8,128)S(1)} %copy-done, f32[8,512,2,64]{3,2,1,0:T(2,128)} %reshape.111), kind=kOutput, calls=%fused_computation.20 | convolution fusion | flops 406257664 | bytes 4284416 | tf_op jit(solution)/shard_map/szuj,cj->szuc/dot_general | solution.py:49
  78.5 1.4 multiply_reduce_fusion
  80.0 0.8 copy.68
  81.2 20.0 %all-gather.3.cloned.1.call-done = f32[4,512,128]{2,1,0:T(8,128)} async-done(((f32[1,512,128]{2,1,0:T(8,128)}), f32[4,512,128]{2,1,0:T(8,128)}) %all-gather.3.cloned.1.call-update) | async-done | bytes 1048592 | tf_op jit(solution)/shard_map/all_gather | solution.py:20
  101.1 1.9 %slice_multiply_fusion.4 = f32[1,512,128]{2,1,0:T(8,128)} fusion(f32[4,512,128]{2,1,0:T(8,128)} %all-gather.3.cloned.1.call-done), kind=kLoop, calls=%fused_computation.27 | loop fusion | flops 196608 | bytes 1310720 | tf_op jit(solution)/shard_map/mul | solution.py:79
  103.7 1.6 %broadcast_in_dim.46 = f32[3,8,64,2,64]{4,3,2,1,0:T(2,128)} broadcast(f32[3,8,2]{2,1,0:T(8,128)S(1)} %copy.72), dimensions={0,1,3} | broadcast | bytes 786624 | tf_op jit(solution)/shard_map/broadcast_in_dim | solution.py:58
  105.4 3.1 %add.64 = f32[3,512,128]{2,1,0:T(8,128)} reshape(f32[3,8,64,2,64]{4,3,2,1,0:T(2,128)} %broadcast_in_dim.46) | data formatting | bytes 1572864 | tf_op jit(solution)/shard_map/add | solution.py:65
  108.5 1.6 %broadcast_in_dim.45 = f32[3,8,64,2,64]{4,3,2,1,0:T(2,128)} broadcast(f32[3,8,2]{2,1,0:T(8,128)S(1)} %copy.70), dimensions={0,1,3} | broadcast | bytes 786624 | tf_op jit(solution)/shard_map/broadcast_in_dim | solution.py:58
  110.2 3.0 %mul.170 = f32[3,512,128]{2,1,0:T(8,128)} reshape(f32[3,8,64,2,64]{4,3,2,1,0:T(2,128)} %broadcast_in_dim.45) | data formatting | bytes 1572864 | tf_op jit(solution)/shard_map/mul | solution.py:65
  113.2 1.8 %copy.71 = f32[8,512,128]{2,1,0:T(8,128)} copy(f32[8,512,128]{1,2,0:T(8,128)S(1)} %bitcast.67) | data formatting | bytes 4194304 | tf_op jit(solution)/shard_map/reshape | solution.py:50
  115.0 4.2 %subtract_multiply_fusion = f32[8,512,128]{1,2,0:T(8,128)} fusion(f32[8,512,128]{1,2,0:T(8,128)S(1)} %bitcast.68, f32[512,128]{0,1:T(8,128)S(1)} %broadcast_in_dim.44, f32[512,128]{0,1:T(8,128)S(1)} %broadcast_in_dim.42, f32[512,128]{0,1:T(8,128)S(1)} %fusion.23), kind=kOutput, calls=%fused_computation.9 | output fusion | flops 15728640 | bytes 4980736 | tf_op jit(solution)/shard_map/jit(cumsum)/reduce_window_sum | solution.py:71
  119.2 3.1 %copy.69 = f32[8,512,128]{2,1,0:T(8,128)} copy(f32[8,512,128]{1,2,0:T(8,128)} %subtract_multiply_fusion) | data formatting | bytes 4194304 | tf_op jit(solution)/shard_map/mul | solution.py:72
  122.3 5.7 %fusion.1 = f32[3,512,128]{2,1,0:T(8,128)S(1)} fusion(f32[3,512,128]{2,1,0:T(8,128)} %add.64, f32[8,512,128]{2,1,0:T(8,128)S(1)} %copy-done.1, f32[3,512,128]{2,1,0:T(8,128)} %mul.170, f32[8,512,128]{2,1,0:T(8,128)} %copy.69), kind=kLoop, calls=%fused_computation.2 | loop fusion | flops 15532032 | bytes 6553600 | tf_op jit(solution)/shard_map/reduce_sum | solution.py:73
  128.0 1.4 slice_multiply_fusion.1
  129.4 7.0 %all_gather.18 = f32[2,512,128]{2,1,0:T(8,128)S(1)} all-gather(f32[1,512,128]{2,1,0:T(8,128)S(1)} %slice_multiply_fusion.1), channel_id=1, replica_groups=mesh['view'=4,'depth_0'=2,'depth_1'=4,'depth_2'=4] {'depth_0'}, dimensions={0}, use_global_device_ids=true | all-gather | bytes 786432 | tf_op jit(solution)/shard_map/all_gather | solution.py:20
  136.8 18.6 %all_to_all.20 = f32[32,3,16,128]{3,2,1,0:T(8,128)S(1)} all-to-all(f32[32,3,16,128]{3,2,1,0:T(8,128)S(1)} %copy.73), channel_id=1, replica_groups=mesh['view'=4,'depth_0'=2,'depth_1'=4,'depth_2'=4] {'depth_0','depth_1',..., dimensions={0} | all-to-all | bytes 1572864 | tf_op jit(solution)/shard_map/all_to_all | solution.py:38
  (45 shorter events, 3.7 us)
Async XLA Ops:
  6.5 65.0 %copy-start = (f32[1,64,64]{2,1,0:T(8,128)S(1)}, f32[1,64,64]{2,1,0:T(8,128)}, u32[]{:S(2)}) copy-start(f32[1,64,64]{2,1,0:T(8,128)} %param.10) | copy-start | bytes 49156
  6.5 5.4 %copy-start.6 = (f32[1,8,64]{2,1,0:T(8,128)S(1)}, f32[1,8,64]{2,1,0:T(8,128)}, u32[]{:S(2)}) copy-start(f32[1,8,64]{2,1,0:T(8,128)} %param.8) | copy-start | bytes 6148
  24.6 10.9 %copy-start.4 = (s32[1,512,128]{2,1,0:T(8,128)S(1)}, s32[1,512,128]{2,1,0:T(8,128)}, u32[]{:S(2)}) copy-start(s32[1,512,128]{2,1,0:T(8,128)} %param.13) | copy-start | bytes 786436
  24.6 11.0 %copy-start.7 = (f32[8,8]{1,0:T(8,128)S(1)}, f32[8,8]{1,0:T(8,128)}, u32[]{:S(2)}) copy-start(f32[8,8]{1,0:T(8,128)} %param.11) | copy-start | bytes 772
  24.6 11.0 %copy-start.8 = (s32[8,2,1]{0,2,1:T(1,128)S(1)}, s32[8,2,1]{0,2,1:T(1,128)}, u32[]{:S(2)}) copy-start(s32[8,2,1]{0,2,1:T(1,128)} %param.12) | copy-start | bytes 196
  24.6 40.4 %all-to-all-start = ((f32[128,8,4,128]{3,1,2,0:T(8,128)}), f32[128,8,4,128]{3,1,2,0:T(8,128)S(1)}, u32[]{:S(2)}, u32[]{:S(2)}) async-start(f32[128,8,4,128]{3,1,2,0:T(8,128)} %bitcast.71), calls=%async_computation | async-start | bytes 4194304 | tf_op jit(solution)/shard_map/all_to_all | solution.py:93
  35.3 65.9 %all-gather.3.cloned.1.call-start = ((), (), s32[]{:S(2)}) async-start(), calls=%async_computation.2 | async-start | bytes 1310720 | tf_op jit(solution)/shard_map/all_gather | solution.py:20
  65.0 0.8 copy-start.5
  80.9 47.1 %all-gather.5.cloned.1.call-start = ((), (), s32[]{:S(2)}) async-start(), calls=%async_computation.3 | async-start | bytes 1310720 | tf_op jit(solution)/shard_map/all_gather | solution.py:20
  119.2 3.1 %copy-start.1 = (f32[8,512,128]{2,1,0:T(8,128)S(1)}, f32[8,512,128]{2,1,0:T(8,128)}, u32[]{:S(2)}) copy-start(f32[8,512,128]{2,1,0:T(8,128)} %copy.71) | copy-start | bytes 6291460
  128.0 8.5 %copy-start.2 = (f32[4,512,128]{2,1,0:T(8,128)S(1)}, f32[4,512,128]{2,1,0:T(8,128)}, u32[]{:S(2)}) copy-start(f32[4,512,128]{2,1,0:T(8,128)} %all-gather.3.cloned.1.call-done) | copy-start | bytes 3145732
  128.0 8.4 %copy-start.3 = (f32[4,512,128]{2,1,0:T(8,128)S(1)}, f32[4,512,128]{2,1,0:T(8,128)}, u32[]{:S(2)}) copy-start(f32[4,512,128]{2,1,0:T(8,128)} %all-gather.5.cloned.1.call-done) | copy-start | bytes 3145732
Sparse Core Ops, SparseCore 0:
  81.0 20.0 all-gather.2
  103.2 24.4 all-gather.4
where the time goes:
time: 163 us
  waiting for transfers between devices  48.8 us (30%)
  blocking collectives  32.9 us (20%)
  local copies, waits for them, and re-layouts  27.7 us (17%)
  other arithmetic  15.6 us (10%)
  between operations  13.6 us (8%)
  matrix products  13.1 us (8%)
  starting transfers between devices  11.1 us (7%)
    all_to_all x1, waiting for transfers between devices, shards(): lax.all_to_all(contracted, VIEW_DEPTH, split_axis=0, concat_axis=2, tiled...  28.8 us
    all_gather x2, waiting for transfers between devices, carried_in(): pieces = lax.all_gather(total, axis)  20 us
    all_to_all x1, blocking collectives, summed_on_arrival(): lax.all_to_all(in_blocks(shard, dim, peers), axis, 0, 0, tiled=True)  18.6 us
    all_to_all x1, starting transfers between devices, shards(): lax.all_to_all(contracted, VIEW_DEPTH, split_axis=0, concat_axis=2, tiled...  10.6 us
    all_gather x1, blocking collectives, shards(): all_weights = lax.all_gather(step_weights, 'view', axis=0, tiled=True)  7.25 us
    dot_general x1, matrix products, finish_brick(): third = jnp.einsum('szuj,cj->szuc', third, cols_map, precision=highest)  7.04 us
    all_gather x1, blocking collectives, carried_in(): pieces = lax.all_gather(total, axis)  7.04 us
    unnamed x20, local copies, waits for them, and re-layouts  5.73 us
  transfers between devices with their start and end apart: 3, of which 2 were waited for; matrix products, arithmetic and copies ran while one was open for 16% of the time, Pallas kernels for 0%

commit v1 on v0

v1 whole, which is shorter than its diff:
```python
import jax
import jax.numpy as jnp
from jax import lax
from jax.experimental import pallas as pl
from jax.experimental.pallas import tpu as pltpu
from jax.sharding import Mesh
from jax.sharding import PartitionSpec as P

AXES = ("zh", "core", "zl", "y", "x")
VIEW = ("zh", "core")
DEPTH = ("zl", "y", "x")
MESH = pl.DeviceIdType.MESH
STEP_LENGTH = 2.0 / 256.0
BF16 = jnp.bfloat16
F32 = jnp.float32


def split(value):
    high = value.astype(BF16)
    low = (value - high.astype(F32)).astype(BF16)
    return high, low


def dot_nt(lhs, rhs):
    return lax.dot_general(lhs, rhs, (((1,), (1,)), ((), ())), preferred_element_type=F32)


def softplus(v):
    return jnp.maximum(v, 0.0) + jnp.log1p(jnp.exp(-jnp.abs(v)))


def step_block(weights):
    twice = jnp.concatenate([weights, weights], axis=1)
    lane = lax.broadcasted_iota(jnp.int32, twice.shape, 1)
    block = jnp.concatenate(
        [jnp.where(lane < 64, twice, 0.0), jnp.where(lane >= 64, twice, 0.0)], axis=0
    )
    high = block.astype(BF16).astype(F32)
    return high, block - high


def step_lhs(weights):
    parts = [step_block(one) for one in weights]
    high = jnp.concatenate([part[0] for part in parts], axis=0)
    low = jnp.concatenate([part[1] for part in parts], axis=0)
    top = jnp.concatenate([high, high], axis=1)
    bottom = jnp.concatenate([low, jnp.zeros_like(low)], axis=1)
    return jnp.concatenate([top, bottom], axis=0).astype(BF16)


def kernel(
    vol, own_w, rows_map, cols_map, table, mats, entry, out,
    cells, sent, got, other_w, row_buf, col_buf, entry_buf, coef_own, coefs,
    row_lhs, col_rhs, second, samples, part, finals,
    cell_sem, send_sem, got_sem, w_send, w_got, map_send, map_got,
    coef_send, coef_got, fin_send, fin_got,
):
    zh, core, zl = lax.axis_index("zh"), lax.axis_index("core"), lax.axis_index("zl")
    y, x = lax.axis_index("y"), lax.axis_index("x")
    place = y * 4 + x
    shift = lax.rem(y - 2 * core - zl + 8, 4)
    mine = lax.rem(2 + 3 * shift, 4)
    view_zh = lax.rem(zh + mine // 2, 2)
    view_core = lax.rem(core + lax.rem(mine, 2), 2)

    def device(zh_=zh, core_=core, zl_=zl, y_=y, x_=x):
        return {"zh": zh_, "core": core_, "zl": zl_, "y": y_, "x": x_}

    def remote(src, dst, send, recv, where):
        return pltpu.make_async_remote_copy(
            src_ref=src, dst_ref=dst, send_sem=send, recv_sem=recv,
            device_id=where, device_id_type=MESH,
        )

    def plane_peer(offset):
        return lax.rem(y + offset // 4, 4), lax.rem(x + lax.rem(offset, 4), 4)

    def view_peer(xor):
        return device(zh_=lax.rem(zh + xor // 2, 2), core_=lax.rem(core + xor % 2, 2))

    octet = zl * 2 + y // 2
    brick_slot = lax.rem(y, 2) * 4 + x
    coef_self = x == octet

    barrier = pltpu.get_barrier_semaphore()

    def greet(where):
        pl.semaphore_signal(barrier, inc=1, device_id=where, device_id_type=MESH)

    @pl.loop(1, 16)
    def _(offset):
        peer_y, peer_x = plane_peer(offset)
        greet(device(y_=peer_y, x_=peer_x))

    for xor in (1, 2, 3):
        greet(view_peer(xor))

    @pl.loop(0, 8)
    def _(i):
        to_zl, to_y = i // 4, lax.rem(i, 4)
        from_y, from_x = 2 * lax.rem(x, 2) + i // 4, lax.rem(i, 4)

        @pl.when(jnp.logical_not(coef_self & (to_zl == zl) & (to_y == y)))
        def _():
            greet(device(zl_=to_zl, y_=to_y, x_=octet))

        @pl.when(jnp.logical_not(coef_self & (from_y == y) & (from_x == x)))
        def _():
            greet(device(zl_=x // 2, y_=from_y, x_=from_x))

    out_y = 2 * core + zl
    source_zh, source_core, source_zl = zl, y // 2, lax.rem(y, 2)
    source_xor = lax.rem(zh + source_zh, 2) * 2 + lax.rem(core + source_core, 2)
    source_y = lax.rem(y + 2 + 3 * source_xor, 4)

    @pl.loop(0, 4)
    def _(i):
        greet(device(view_zh, view_core, zh, out_y, i))
        greet(device(source_zh, source_core, source_zl, source_y, i))

    def cell_copy(rho, q):
        return pltpu.make_async_copy(
            vol.at[:, :, pl.ds(512 * q + 128 * rho, 128)], cells.at[rho, q], cell_sem.at[rho, q]
        )

    for rho in range(4):
        for q in range(4):
            cell_copy(rho, q).start()

    def contract(lhs, rho, q, first_view, count):
        high, low = split(cells[rho, q].reshape(512, 128))
        wide = dot_nt(lhs, jnp.concatenate([high, low], axis=1))
        wide = wide[: 16 * count] + wide[16 * count :]
        for k in range(count):
            for pair in range(2):
                for z in range(4):
                    row = 16 * k + 8 * pair
                    sent[(first_view + k) * 4 + q, 2 * rho + pair, pl.ds(8 * z, 8), :] = wide[
                        row : row + 8, 128 * z : 128 * z + 128
                    ]

    def send_brick(j, offset):
        peer_y, peer_x = plane_peer(offset)
        peer_shift = lax.rem(peer_y - 2 * core - zl + 8, 4)
        slot = lax.rem(2 + 3 * peer_shift, 4) * 4 + peer_x
        return remote(
            sent.at[slot, j], got.at[j, pl.ds(32 * place, 32)], send_sem.at[0], got_sem.at[j],
            device(y_=peer_y, x_=peer_x),
        )

    def peer_xor(offset):
        peer_y, _ = plane_peer(offset)
        return lax.rem(2 + 3 * lax.rem(peer_y - 2 * core - zl + 8, 4), 4)

    own_lhs = step_lhs([own_w[0]])
    for rho in range(4):
        for q in range(4):
            cell_copy(rho, q).wait()
            contract(own_lhs, rho, q, 0, 1)

    lane = lax.broadcasted_iota(jnp.int32, (8, 128), 1)
    sublane = lax.broadcasted_iota(jnp.int32, (8, 128), 0)
    for k in range(2):
        tile = 2 * (2 * zh + core) + k
        wanted = jnp.where(lane < 64, mats[tile, 0, 0], mats[tile, 1, 0])
        onehot = (sublane == wanted).astype(F32)
        coef_own[k] = lax.dot_general(
            table[...], onehot, (((0,), (0,)), ((), ())),
            precision=lax.Precision.HIGHEST, preferred_element_type=F32,
        )

    @pl.when(coef_self)
    def _():
        coefs[brick_slot] = coef_own[zl]

    pl.semaphore_wait(barrier, 42 - 2 * coef_self.astype(jnp.int32))

    w_copies = [
        remote(own_w.at[0], other_w.at[xor], w_send.at[xor], w_got.at[xor], view_peer(xor))
        for xor in (1, 2, 3)
    ]
    for copy in w_copies:
        copy.start()

    @pl.loop(0, 8)
    def _(j):
        @pl.loop(1, 16)
        def _(offset):
            @pl.when(peer_xor(offset) == 0)
            def _():
                send_brick(j, offset).start()

    turned = lax.rem(shift, 2) == 1
    to_xor = jnp.where(turned, lax.rem(2 + 3 * (shift + 2), 4), mine)
    to_zh, to_core = lax.rem(zh + to_xor // 2, 2), lax.rem(core + lax.rem(to_xor, 2), 2)
    to_rows = pl.multiple_of((2 * (2 * to_zh + to_core) + zl) * 64, 64)
    to_device = device(zh_=to_zh, core_=to_core)
    maps = (
        (rows_map.at[0], row_buf),
        (cols_map.at[0], col_buf),
        (entry.at[0, pl.ds(to_rows, 64)], entry_buf),
    )

    @pl.when(mine == 0)
    def _():
        for i, (src, dst) in enumerate(maps):
            pltpu.make_async_copy(src, dst, map_got.at[i]).start()

    @pl.when(mine != 0)
    def _():
        for i, (src, dst) in enumerate(maps):
            remote(src, dst, map_send.at[i], map_got.at[i], to_device).start()

    def coef_copy(i):
        to_zl, to_y = i // 4, lax.rem(i, 4)
        return remote(
            coef_own.at[to_zl], coefs.at[brick_slot], coef_send.at[0], coef_got.at[0],
            device(zl_=to_zl, y_=to_y, x_=octet),
        )

    @pl.loop(0, 8)
    def _(i):
        @pl.when(jnp.logical_not(coef_self & (i // 4 == zl) & (lax.rem(i, 4) == y)))
        def _():
            coef_copy(i).start()

    for copy in w_copies:
        copy.wait()
    lhs = step_lhs([other_w[1], other_w[2], other_w[3]])
    for rho in range(4):
        for q in range(4):
            contract(lhs, rho, q, 1, 3)

        for pair in range(2):
            @pl.loop(1, 16)
            def _(offset, j=2 * rho + pair):
                @pl.when(peer_xor(offset) != 0)
                def _():
                    send_brick(j, offset).start()

    own_slot = mine * 4 + x

    @pl.loop(0, 8)
    def _(j):
        got[j, pl.ds(pl.multiple_of(32 * place, 32), 32), :] = sent[own_slot, j]

    for i, (src, dst) in enumerate(maps):
        pltpu.make_async_copy(src, dst, map_got.at[i]).wait()

    row_map = row_buf[...]
    row_high = row_map.astype(BF16).astype(F32)
    row_lhs[...] = jnp.concatenate([row_high, row_high, row_map - row_high], axis=1).astype(BF16)
    col_map = col_buf[...]
    none = jnp.zeros_like(col_map)
    col_block = jnp.concatenate(
        [jnp.concatenate([col_map, none], axis=1), jnp.concatenate([none, col_map], axis=1)], axis=0
    )
    col_high, col_low = split(col_block)
    col_rhs[...] = jnp.concatenate(
        [
            jnp.concatenate([col_high, col_high], axis=1),
            jnp.concatenate([col_low, jnp.zeros_like(col_low)], axis=1),
        ],
        axis=0,
    )

    @pl.when(coef_self)
    def _():
        pltpu.make_async_copy(coefs.at[pl.ds(0, 7)], coefs.at[pl.ds(0, 7)], coef_got.at[0]).wait()

    @pl.when(jnp.logical_not(coef_self))
    def _():
        pltpu.make_async_copy(coefs, coefs, coef_got.at[0]).wait()

    part[0:3] = jnp.zeros((3, 64, 128), F32)
    part[3] = jnp.ones((64, 128), F32)

    @pl.loop(0, 8)
    def _(j):
        waited = got.at[j, pl.ds(0, 480)]
        pltpu.make_async_copy(waited, waited, got_sem.at[j]).wait()
        for pair in range(4):
            both = jnp.concatenate(
                [got[j, pl.ds(2 * pair + k, 64, stride=8), :] for k in range(2)], axis=1
            )
            high, low = split(both)
            rows = jnp.dot(
                row_lhs[...], jnp.concatenate([high, low, high], axis=0), preferred_element_type=F32
            )
            for k in range(2):
                high, low = split(rows[:, 128 * k : 128 * k + 128])
                at = pl.ds((2 * pair + k) * 64, 64)
                second[at, 0:128] = high
                second[at, 128:256] = low
        wide = dot_nt(second[...], col_rhs[...])
        samples[...] = wide[:, 0:128] + wide[:, 128:256]
        coef = coefs[j]

        @pl.loop(0, 2)
        def _(block):
            at = pl.multiple_of(block * 32, 32)
            rows = pl.ds(at, 32)
            live = entry_buf[rows, :] <= 8 * x + j
            red, green, blue, through = part[0, rows], part[1, rows], part[2, rows], part[3, rows]
            for s in range(8):
                value = samples[pl.ds(at + 64 * s, 32), :]
                tau = STEP_LENGTH * softplus(coef[6:7] * value + coef[7:8])
                kept = jnp.exp(-jnp.where(live, tau, 0.0))
                weight = through * (1.0 - kept)
                through = through * kept
                red = red + weight * softplus(coef[0:1] * value + coef[3:4])
                green = green + weight * softplus(coef[1:2] * value + coef[4:5])
                blue = blue + weight * softplus(coef[2:3] * value + coef[5:6])
            part[0, rows], part[1, rows], part[2, rows], part[3, rows] = red, green, blue, through

    def final_copy(i):
        return remote(
            part.at[:, pl.ds(16 * i, 16)], finals.at[x], fin_send.at[i], fin_got.at[0],
            device(view_zh, view_core, zh, out_y, i),
        )

    for i in range(4):
        final_copy(i).start()
    pltpu.make_async_copy(finals, finals, fin_got.at[0]).wait()
    total = finals[3, 0:3]
    for q in (2, 1, 0):
        total = finals[q, 0:3] + finals[q, 3:4] * total
    out[0] = total

    for i in range(4):
        final_copy(i).wait_send()
    drained = sent.at[pl.ds(0, 15)]
    pltpu.make_async_copy(drained, drained, send_sem.at[0]).wait()

    @pl.when(mine != 0)
    def _():
        for i, (src, dst) in enumerate(maps):
            remote(src, dst, map_send.at[i], map_got.at[i], to_device).wait_send()

    @pl.when(coef_self)
    def _():
        pltpu.make_async_copy(coefs.at[pl.ds(0, 7)], coefs.at[pl.ds(0, 7)], coef_send.at[0]).wait()

    @pl.when(jnp.logical_not(coef_self))
    def _():
        pltpu.make_async_copy(coefs, coefs, coef_send.at[0]).wait()


def render(volume, step_weights, row_interp, col_interp, tf_table, materials, entry):
    vmem = pl.BlockSpec(memory_space=pltpu.VMEM)
    anywhere = pl.BlockSpec(memory_space=pl.ANY)
    smem = pl.BlockSpec(memory_space=pltpu.SMEM)
    dma = pltpu.SemaphoreType.DMA
    return pl.pallas_call(
        kernel,
        name="render",
        out_shape=jax.ShapeDtypeStruct((1, 3, 16, 128), F32),
        in_specs=[anywhere, vmem, anywhere, anywhere, vmem, smem, anywhere],
        out_specs=vmem,
        scratch_shapes=[
            pltpu.VMEM((4, 4, 4, 128, 128), F32),
            pltpu.VMEM((16, 8, 32, 128), F32),
            pltpu.VMEM((8, 512, 128), F32),
            pltpu.VMEM((4, 8, 64), F32),
            pltpu.VMEM((64, 64), F32),
            pltpu.VMEM((64, 64), F32),
            pltpu.VMEM((64, 128), jnp.int32),
            pltpu.VMEM((2, 8, 128), F32),
            pltpu.VMEM((8, 8, 128), F32),
            pltpu.VMEM((64, 192), BF16),
            pltpu.VMEM((256, 256), BF16),
            pltpu.VMEM((512, 256), BF16),
            pltpu.VMEM((512, 128), F32),
            pltpu.VMEM((4, 64, 128), F32),
            pltpu.VMEM((4, 4, 16, 128), F32),
            dma((4, 4)), dma((1,)), dma((8,)), dma((4,)), dma((4,)), dma((3,)), dma((3,)),
            dma((1,)), dma((1,)), dma((4,)), dma((1,)),
        ],
        compiler_params=pltpu.CompilerParams(
            collective_id=0, has_side_effects=True, vmem_limit_bytes=60 * 1024 * 1024
        ),
    )(volume, step_weights, row_interp, col_interp, tf_table, materials, entry)


def solution(mesh):
    torus = Mesh(mesh.devices.reshape(2, 2, 2, 4, 4), AXES)
    return jax.shard_map(
        render,
        mesh=torus,
        in_specs=(
            P(AXES, None, None),
            P(VIEW, None, None),
            P(VIEW, None, None),
            P(VIEW, None, None),
            P(),
            P(None, None, DEPTH),
            P(VIEW, None, None),
        ),
        out_specs=P(VIEW, None, DEPTH, None),
        check_vma=False,
    )
```

time: 163 us -> 56.3 us (0.35)
  the two profiles are of different devices: /device:TPU:0 before, /device:TPU:33 now
where the time goes in v1:
time: 56.3 us; the launch traced here: 56.1 us
  Pallas kernels  53.4 us (95%)
  local copies, waits for them, and re-layouts  2.7 us (5%)
    pallas_call x1, Pallas kernels, render(): pl.pallas_call(kernel, name='render', out_shape=jax.ShapeDtypeStruct((1,...  53.4 us
    unnamed x2, local copies, waits for them, and re-layouts  2.7 us

profile of v1, /device:TPU:33, one launch (start us, length us, event | category | flops | bytes accessed | tf_op | source)
XLA Modules:
  0.0 56.1 jit_solution(14563546212976692623)
XLA Ops:
  0.0 1.4 %copy.8.mats = s32[8,2,1]{2,1,0:T(2,128)} copy(s32[8,2,1]{0,2,1:T(1,128)} %param.12) | data formatting | bytes 128 | tf_op args[5]
  1.4 53.4 %render.1 = f32[1,3,16,128]{3,2,1,0:T(8,128)} custom-call(f32[4,128,2048]{2,1,0:T(8,128)} %vol.1, f32[1,8,64]{2,1,0:T(8,128)} %own_w.1, f32[1,64,64]{2,1,0:T(8,128)} %rows_map.1, f32[1,64,64]{2,1,0:T(8,128)} %cols_map.1, f32[8,8]{1,0:T(8,128)} %table.1, s32[8,2,1]{2,1,0:T(2,128)} %copy.8.mats, s32[1,512,128]{2,1,0:T(8,128)} %entry.1), custom_call_target="tpu_custom_call" | custom-call | tf_op jit(solution)/shard_map/render/pallas_call | solution.py:354
  54.8 1.3 %copy.10 = f32[1,3,16,128]{3,2,1,0:T(8,128)} copy(f32[1,3,16,128]{3,2,1,0:T(8,128)} %render.1) | data formatting | bytes 49152

commit v2 on v1

v2 whole, which is shorter than its diff:
```python
import jax
import jax.numpy as jnp
from jax import lax
from jax.experimental import pallas as pl
from jax.experimental.pallas import tpu as pltpu
from jax.sharding import Mesh
from jax.sharding import PartitionSpec as P

AXES = ("zh", "core", "zl", "y", "x")
VIEW = ("zh", "core")
DEPTH = ("zl", "y", "x")
MESH = pl.DeviceIdType.MESH
STEP_LENGTH = 2.0 / 256.0
LOG2E = 1.4426950408889634
LN2 = 0.6931471805599453
BF16 = jnp.bfloat16
F32 = jnp.float32


def split(value):
    high = value.astype(BF16)
    low = (value - high.astype(F32)).astype(BF16)
    return high, low


def dot_nt(lhs, rhs):
    return lax.dot_general(lhs, rhs, (((1,), (1,)), ((), ())), preferred_element_type=F32)


def softplus2(v):
    power = jnp.exp2(jnp.minimum(v, 64.0))
    grown = 1.0 + power
    return jnp.maximum(v, jnp.log2(grown) + LOG2E * (power - (grown - 1.0)))


def step_block(weights):
    twice = jnp.concatenate([weights, weights], axis=1)
    lane = lax.broadcasted_iota(jnp.int32, twice.shape, 1)
    block = jnp.concatenate(
        [jnp.where(lane < 64, twice, 0.0), jnp.where(lane >= 64, twice, 0.0)], axis=0
    )
    high = block.astype(BF16).astype(F32)
    return high, block - high


def step_lhs(weights):
    parts = [step_block(one) for one in weights]
    high = jnp.concatenate([part[0] for part in parts], axis=0)
    low = jnp.concatenate([part[1] for part in parts], axis=0)
    top = jnp.concatenate([high, high], axis=1)
    bottom = jnp.concatenate([low, jnp.zeros_like(low)], axis=1)
    return jnp.concatenate([top, bottom], axis=0).astype(BF16)


ROUNDS = ((0, 2), (2, 2), (4, 2), (6, 1), (7, 1))


def kernel(
    vol, step_map, rows_map, cols_map, table_in, mats_in, entry, out,
    cells, sent, got, weights, table, mats, row_buf, col_buf, entry_buf, coef_own, coef_relay, coefs,
    row_lhs, col_rhs, second, samples, part, finals,
    cell_sem, small_sem, send_sem, got_sem, w_send, w_got, map_send, map_got,
    coef_send, coef_got, pair_send, pair_got, fin_send, fin_got,
):
    zh, core, zl = lax.axis_index("zh"), lax.axis_index("core"), lax.axis_index("zl")
    y, x = lax.axis_index("y"), lax.axis_index("x")

    def cell_copy(rho, q):
        return pltpu.make_async_copy(
            vol.at[:, :, pl.ds(512 * q + 128 * rho, 128)], cells.at[rho, q], cell_sem.at[rho, q]
        )

    small = [
        pltpu.make_async_copy(step_map.at[0], weights.at[0], small_sem.at[0]),
        pltpu.make_async_copy(mats_in, mats, small_sem.at[1]),
        pltpu.make_async_copy(table_in, table, small_sem.at[2]),
    ]
    for copy in small:
        copy.start()
    for rho in range(4):
        for q in range(4):
            cell_copy(rho, q).start()

    place = y * 4 + x
    shift = lax.rem(y - 2 * core - zl + 8, 4)
    mine = lax.rem(2 + 3 * shift, 4)
    view_zh, view_core = lax.rem(zh + mine // 2, 2), lax.rem(core + lax.rem(mine, 2), 2)
    out_y = 2 * core + zl

    def device(zh_=zh, core_=core, zl_=zl, y_=y, x_=x):
        return {"zh": zh_, "core": core_, "zl": zl_, "y": y_, "x": x_}

    def remote(src, dst, send, recv, where):
        return pltpu.make_async_remote_copy(
            src_ref=src, dst_ref=dst, send_sem=send, recv_sem=recv,
            device_id=where, device_id_type=MESH,
        )

    def view_peer(xor):
        return device(zh_=lax.rem(zh + xor // 2, 2), core_=lax.rem(core + xor % 2, 2))

    def take(ref, sem):
        pltpu.make_async_copy(ref, ref, sem).wait()

    brick_slot = lax.rem(y, 2) * 4 + x
    coef_self = lax.rem(x, 2) == y // 2
    barrier = pltpu.get_barrier_semaphore()

    def greet(where):
        pl.semaphore_signal(barrier, inc=1, device_id=where, device_id_type=MESH)

    with jax.named_scope("greet"):
        for xor in (1, 2, 3):
            greet(view_peer(xor))
        for offset in range(15, 0, -1):
            greet(device(y_=lax.rem(y + offset // 4, 4), x_=lax.rem(x + offset % 4, 4)))
        greet(device(zl_=1 - zl))

    def contract(lhs, rho, q, first_view, count):
        high, low = split(cells[rho, q].reshape(512, 128))
        wide = dot_nt(lhs, jnp.concatenate([high, low], axis=1))
        wide = wide[: 16 * count] + wide[16 * count :]
        for k in range(count):
            for pair in range(2):
                for z in range(4):
                    row = 16 * k + 8 * pair
                    sent[(first_view + k) * 4 + q, 2 * rho + pair, pl.ds(8 * z, 8), :] = wide[
                        row : row + 8, 128 * z : 128 * z + 128
                    ]

    def plane_copy(xor, column, first, count, sem):
        peer_y = lax.rem((2 + 3 * xor) % 4 + 2 * core + zl, 4)
        copy = remote(
            sent.at[4 * xor + column, pl.ds(first, count)],
            got.at[pl.ds(first, count), pl.ds(pl.multiple_of(32 * place, 32), 32)],
            send_sem.at[sem], got_sem.at[sem], device(y_=peer_y, x_=column),
        )
        pl.when(jnp.logical_not((mine == xor) & (x == column)))(copy.start)

    def send_round(number, columns=range(4)):
        for xor in range(4):
            for column in columns:
                plane_copy(xor, column, *ROUNDS[number], number)

    def sent_round(number):
        first, count = ROUNDS[number]
        take(sent.at[pl.ds(0, 15), pl.ds(first, count)], send_sem.at[number])

    def send_coefs(plane, source):
        column = plane * 2 + y // 2
        for row in range(4):
            here = (row == y) & (column == x)
            copy = remote(
                source, coefs.at[brick_slot], coef_send.at[0], coef_got.at[0],
                device(y_=row, x_=column),
            )
            pl.when(jnp.logical_not(here))(copy.start)

            @pl.when(here)
            def _():
                coefs[brick_slot] = source[...]

    partner_copy = remote(
        coef_own.at[1 - zl], coef_relay, pair_send.at[0], pair_got.at[0], device(zl_=1 - zl)
    )
    w_copies = [
        remote(weights.at[0], weights.at[xor], w_send.at[xor], w_got.at[xor], view_peer(xor))
        for xor in (1, 2, 3)
    ]
    with jax.named_scope("small"):
        small[0].wait()
    with jax.named_scope("meet"):
        pl.semaphore_wait(barrier, 19)
    for copy in w_copies:
        copy.start()
    with jax.named_scope("classes"):
        for copy in small[1:]:
            copy.wait()
        lane = lax.broadcasted_iota(jnp.int32, (8, 128), 1)
        sublane = lax.broadcasted_iota(jnp.int32, (8, 128), 0)
        for k in range(2):
            tile = 2 * (2 * zh + core) + k
            wanted = jnp.where(lane < 64, mats[0, 0, tile], mats[1, 0, tile])
            onehot = (sublane == wanted).astype(F32)
            coef_own[k] = lax.dot_general(
                table[...], onehot, (((0,), (0,)), ((), ())),
                precision=lax.Precision.HIGHEST, preferred_element_type=F32,
            )
        partner_copy.start()
        send_coefs(zl, coef_own.at[zl])
    own_lhs = step_lhs([weights[0]])
    for rho in range(4):
        with jax.named_scope("wait_cells"):
            for q in range(4):
                cell_copy(rho, q).wait()
        with jax.named_scope("own_view"):
            for q in range(4):
                contract(own_lhs, rho, q, 0, 1)
    to_xor = jnp.where(lax.rem(shift, 2) == 1, lax.rem(2 + 3 * (shift + 2), 4), mine)
    to_zh, to_core = lax.rem(zh + to_xor // 2, 2), lax.rem(core + lax.rem(to_xor, 2), 2)
    to_rows = pl.multiple_of((2 * (2 * to_zh + to_core) + zl) * 64, 64)
    to_device = device(zh_=to_zh, core_=to_core)
    maps = (
        (rows_map.at[0], row_buf),
        (cols_map.at[0], col_buf),
        (entry.at[0, pl.ds(to_rows, 64)], entry_buf),
    )

    with jax.named_scope("wait_weights"):
        for copy in w_copies:
            copy.wait()
    with jax.named_scope("relay"):
        partner_copy.wait()
        send_coefs(1 - zl, coef_relay)
    lhs = step_lhs([weights[xor] for xor in (1, 2, 3)])
    for rho in range(4):
        with jax.named_scope("contract"):
            for q in range(4):
                contract(lhs, rho, q, 1, 3)
                if rho == 0:
                    send_round(0, (q,))
        if rho > 0:
            with jax.named_scope("send_round"):
                for number, (first, _) in enumerate(ROUNDS):
                    if first // 2 == rho:
                        send_round(number)

    @pl.when(mine == 0)
    def _():
        for i, (src, dst) in enumerate(maps):
            pltpu.make_async_copy(src, dst, map_got.at[i]).start()

    @pl.when(mine != 0)
    def _():
        for i, (src, dst) in enumerate(maps):
            remote(src, dst, map_send.at[i], map_got.at[i], to_device).start()

    own_slot = 4 * mine + x

    @pl.loop(0, 8)
    def _(j):
        got[j, pl.ds(pl.multiple_of(32 * place, 32), 32), :] = sent[own_slot, j]

    with jax.named_scope("wait_maps"):
        for i, (src, dst) in enumerate(maps):
            pltpu.make_async_copy(src, dst, map_got.at[i]).wait()

    row_map = row_buf[...]
    row_high = row_map.astype(BF16).astype(F32)
    row_lhs[...] = jnp.concatenate([row_high, row_high, row_map - row_high], axis=1).astype(BF16)
    col_map = col_buf[...]
    none = jnp.zeros_like(col_map)
    col_block = jnp.concatenate(
        [jnp.concatenate([col_map, none], axis=1), jnp.concatenate([none, col_map], axis=1)], axis=0
    )
    col_high, col_low = split(col_block)
    col_rhs[...] = jnp.concatenate(
        [
            jnp.concatenate([col_high, col_high], axis=1),
            jnp.concatenate([col_low, jnp.zeros_like(col_low)], axis=1),
        ],
        axis=0,
    )

    def coef_done(sem):
        pl.when(coef_self)(lambda: take(coefs.at[pl.ds(0, 7)], sem))
        pl.when(jnp.logical_not(coef_self))(lambda: take(coefs, sem))

    with jax.named_scope("wait_classes"):
        coef_done(coef_got.at[0])

    part[0:3] = jnp.zeros((3, 64, 128), F32)
    part[3] = jnp.ones((64, 128), F32)

    def render_brick(j):
        for pair in range(4):
            both = jnp.concatenate(
                [got[j, pl.ds(2 * pair + k, 64, stride=8), :] for k in range(2)], axis=1
            )
            high, low = split(both)
            rows = jnp.dot(
                row_lhs[...], jnp.concatenate([high, low, high], axis=0), preferred_element_type=F32
            )
            for k in range(2):
                high, low = split(rows[:, 128 * k : 128 * k + 128])
                at = pl.ds((2 * pair + k) * 64, 64)
                second[at, 0:128] = high
                second[at, 128:256] = low
        wide = dot_nt(second[...], col_rhs[...])
        samples[...] = wide[:, 0:128] + wide[:, 128:256]
        coef = LOG2E * coefs[j]

        @pl.loop(0, 2)
        def _(block):
            at = pl.multiple_of(block * 32, 32)
            rows = pl.ds(at, 32)
            opacity = jnp.where(entry_buf[rows, :] <= 8 * x + j, -STEP_LENGTH, 0.0)
            red, green, blue, through = part[0, rows], part[1, rows], part[2, rows], part[3, rows]
            for s in range(8):
                value = samples[pl.ds(at + 64 * s, 32), :]
                after = through * jnp.exp2(opacity * softplus2(coef[6:7] * value + coef[7:8]))
                weight = through - after
                through = after
                red = red + weight * softplus2(coef[0:1] * value + coef[3:4])
                green = green + weight * softplus2(coef[1:2] * value + coef[4:5])
                blue = blue + weight * softplus2(coef[2:3] * value + coef[5:6])
            part[0, rows], part[1, rows], part[2, rows], part[3, rows] = red, green, blue, through

    for number, (first, count) in enumerate(ROUNDS):
        with jax.named_scope("wait_brick"):
            take(got.at[pl.ds(first, count), pl.ds(0, 480)], got_sem.at[number])
        with jax.named_scope("bricks"):
            pl.loop(first, first + count)(render_brick)

    def final_copy(i):
        return remote(
            part.at[:, pl.ds(16 * i, 16)], finals.at[x], fin_send.at[i], fin_got.at[0],
            device(view_zh, view_core, zh, out_y, i),
        )

    for i in range(4):
        final_copy(i).start()
    with jax.named_scope("wait_finals"):
        take(finals, fin_got.at[0])
    total = finals[3, 0:3]
    for q in (2, 1, 0):
        total = finals[q, 0:3] + finals[q, 3:4] * total
    out[0] = LN2 * total

    for i in range(4):
        final_copy(i).wait_send()
    with jax.named_scope("drain"):
        for number in range(len(ROUNDS)):
            sent_round(number)

    @pl.when(mine != 0)
    def _():
        for i, (src, dst) in enumerate(maps):
            remote(src, dst, map_send.at[i], map_got.at[i], to_device).wait_send()

    coef_done(coef_send.at[0])


def render(volume, step_weights, row_interp, col_interp, tf_table, materials, entry):
    vmem = pl.BlockSpec(memory_space=pltpu.VMEM)
    anywhere = pl.BlockSpec(memory_space=pl.ANY)
    dma = pltpu.SemaphoreType.DMA
    return pl.pallas_call(
        kernel,
        name="render",
        out_shape=pltpu.VMEM((1, 3, 16, 128), F32),
        in_specs=[anywhere] * 7,
        out_specs=vmem,
        scratch_shapes=[
            pltpu.VMEM((4, 4, 4, 128, 128), F32),
            pltpu.VMEM((16, 8, 32, 128), F32),
            pltpu.VMEM((8, 512, 128), F32),
            pltpu.VMEM((4, 8, 64), F32),
            pltpu.VMEM((8, 8), F32),
            pltpu.SMEM((2, 1, 8), jnp.int32),
            pltpu.VMEM((64, 64), F32),
            pltpu.VMEM((64, 64), F32),
            pltpu.VMEM((64, 128), jnp.int32),
            pltpu.VMEM((2, 8, 128), F32),
            pltpu.VMEM((8, 128), F32),
            pltpu.VMEM((8, 8, 128), F32),
            pltpu.VMEM((64, 192), BF16),
            pltpu.VMEM((256, 256), BF16),
            pltpu.VMEM((512, 256), BF16),
            pltpu.VMEM((512, 128), F32),
            pltpu.VMEM((4, 64, 128), F32),
            pltpu.VMEM((4, 4, 16, 128), F32),
            dma((4, 4)), dma((3,)), dma((5,)), dma((5,)), dma((4,)), dma((4,)), dma((3,)), dma((3,)),
            dma((1,)), dma((1,)), dma((1,)), dma((1,)), dma((4,)), dma((1,)),
        ],
        compiler_params=pltpu.CompilerParams(
            collective_id=0, has_side_effects=True, vmem_limit_bytes=60 * 1024 * 1024
        ),
    )(
        volume, step_weights, row_interp, col_interp, tf_table, materials.transpose(1, 2, 0), entry
    )


def solution(mesh):
    torus = Mesh(mesh.devices.reshape(2, 2, 2, 4, 4), AXES)
    return jax.shard_map(
        render,
        mesh=torus,
        in_specs=(
            P(AXES, None, None),
            P(VIEW, None, None),
            P(VIEW, None, None),
            P(VIEW, None, None),
            P(),
            P(None, None, DEPTH),
            P(VIEW, None, None),
        ),
        out_specs=P(VIEW, None, DEPTH, None),
        check_vma=False,
    )
```

time: 56.3 us -> 45.1 us (0.80)
  the two profiles are of different devices: /device:TPU:33 before, /device:TPU:1 now
where the time goes in v2:
time: 45.1 us; the launch traced here: 44.7 us
  Pallas kernels  44 us (98%)
  local copies, waits for them, and re-layouts  0.61 us (1%)
    pallas_call x1, Pallas kernels, render(): pl.pallas_call(kernel, name='render', out_shape=pltpu.VMEM((1, 3, 16, 128...  44 us

profile of v2, /device:TPU:1, one launch (start us, length us, event | category | flops | bytes accessed | tf_op | source)
XLA Modules:
  0.0 44.7 jit_solution(14704265614265604161)
XLA Ops:
  0.0 44.0 %render.1 = f32[1,3,16,128]{3,2,1,0:T(8,128)S(1)} custom-call(f32[4,128,2048]{2,1,0:T(8,128)} %vol.1, f32[1,8,64]{2,1,0:T(8,128)} %step_map.1, f32[1,64,64]{2,1,0:T(8,128)} %rows_map.1, f32[1,64,64]{2,1,0:T(8,128)} %cols_map.1, f32[8,8]{1,0:T(8,128)} %table_in.1, s32[2,1,8]{2,1,0:T(1,128)} %bitcast.1, s32[1,512,128]{2,1,0:T(8,128)} %entry.1), custom_call_target="tpu_custom_call" | custom-call | tf_op jit(solution)/shard_map/render/pallas_call | solution.py:348
  44.0 0.6 %copy.9 = f32[1,3,16,128]{3,2,1,0:T(8,128)} copy(f32[1,3,16,128]{3,2,1,0:T(8,128)S(1)} %render.1) | data formatting | bytes 49152

commit v3 on v2

--- a/solution.py
+++ b/solution.py
@@ -60,7 +60,7 @@
     cells, sent, got, weights, table, mats, row_buf, col_buf, entry_buf, coef_own, coef_relay, coefs,
     row_lhs, col_rhs, second, samples, part, finals,
     cell_sem, small_sem, send_sem, got_sem, w_send, w_got, map_send, map_got,
-    coef_send, coef_got, pair_send, pair_got, fin_send, fin_got,
+    coef_send, coef_got, pair_send, pair_got, fin_send, fin_got, row_ready, plane_ready,
 ):
     zh, core, zl = lax.axis_index("zh"), lax.axis_index("core"), lax.axis_index("zl")
     y, x = lax.axis_index("y"), lax.axis_index("x")
@@ -77,9 +77,6 @@
     ]
     for copy in small:
         copy.start()
-    for rho in range(4):
-        for q in range(4):
-            cell_copy(rho, q).start()
 
     place = y * 4 + x
     shift = lax.rem(y - 2 * core - zl + 8, 4)
@@ -109,12 +106,15 @@
     def greet(where):
         pl.semaphore_signal(barrier, inc=1, device_id=where, device_id_type=MESH)
 
+    rows = [device(x_=lax.rem(x + i, 4)) for i in (2, 1, 3)]
+    columns = [device(y_=lax.rem(y + i, 4)) for i in (2, 1, 3)]
+    pair = device(zl_=1 - zl)
     with jax.named_scope("greet"):
-        for xor in (1, 2, 3):
-            greet(view_peer(xor))
-        for offset in range(15, 0, -1):
-            greet(device(y_=lax.rem(y + offset // 4, 4), x_=lax.rem(x + offset % 4, 4)))
-        greet(device(zl_=1 - zl))
+        for peer in [view_peer(2), view_peer(3)] + rows + columns + [pair, view_peer(1)]:
+            greet(peer)
+    for rho in range(4):
+        for q in range(4):
+            cell_copy(rho, q).start()
 
     def contract(lhs, rho, q, first_view, count):
         high, low = split(cells[rho, q].reshape(512, 128))
@@ -161,7 +161,7 @@
                 coefs[brick_slot] = source[...]
 
     partner_copy = remote(
-        coef_own.at[1 - zl], coef_relay, pair_send.at[0], pair_got.at[0], device(zl_=1 - zl)
+        coef_own.at[1 - zl], coef_relay, pair_send.at[0], pair_got.at[0], pair
     )
     w_copies = [
         remote(weights.at[0], weights.at[xor], w_send.at[xor], w_got.at[xor], view_peer(xor))
@@ -170,9 +170,11 @@
     with jax.named_scope("small"):
         small[0].wait()
     with jax.named_scope("meet"):
-        pl.semaphore_wait(barrier, 19)
+        pl.semaphore_wait(barrier, 10)
     for copy in w_copies:
         copy.start()
+    for peer in columns:
+        pl.semaphore_signal(row_ready, inc=1, device_id=peer, device_id_type=MESH)
     with jax.named_scope("classes"):
         for copy in small[1:]:
             copy.wait()
@@ -187,15 +189,24 @@
                 precision=lax.Precision.HIGHEST, preferred_element_type=F32,
             )
         partner_copy.start()
-        send_coefs(zl, coef_own.at[zl])
     own_lhs = step_lhs([weights[0]])
-    for rho in range(4):
+
+    def own_view(rho):
         with jax.named_scope("wait_cells"):
             for q in range(4):
                 cell_copy(rho, q).wait()
         with jax.named_scope("own_view"):
             for q in range(4):
                 contract(own_lhs, rho, q, 0, 1)
+
+    own_view(0)
+    own_view(1)
+    with jax.named_scope("plane"):
+        pl.semaphore_wait(row_ready, 3)
+    pl.semaphore_signal(plane_ready, inc=1, device_id=pair, device_id_type=MESH)
+    send_coefs(zl, coef_own.at[zl])
+    own_view(2)
+    own_view(3)
     to_xor = jnp.where(lax.rem(shift, 2) == 1, lax.rem(2 + 3 * (shift + 2), 4), mine)
     to_zh, to_core = lax.rem(zh + to_xor // 2, 2), lax.rem(core + lax.rem(to_xor, 2), 2)
     to_rows = pl.multiple_of((2 * (2 * to_zh + to_core) + zl) * 64, 64)
@@ -209,21 +220,25 @@
     with jax.named_scope("wait_weights"):
         for copy in w_copies:
             copy.wait()
-    with jax.named_scope("relay"):
-        partner_copy.wait()
-        send_coefs(1 - zl, coef_relay)
     lhs = step_lhs([weights[xor] for xor in (1, 2, 3)])
     for rho in range(4):
         with jax.named_scope("contract"):
-            for q in range(4):
+            for i in range(4):
+                q = lax.rem(x + i, 4) if rho == 0 else i
                 contract(lhs, rho, q, 1, 3)
                 if rho == 0:
                     send_round(0, (q,))
+        if rho == 0:
+            with jax.named_scope("relay"):
+                partner_copy.wait()
+                send_coefs(1 - zl, coef_relay)
         if rho > 0:
             with jax.named_scope("send_round"):
                 for number, (first, _) in enumerate(ROUNDS):
                     if first // 2 == rho:
                         send_round(number)
+
+    pl.semaphore_wait(plane_ready, 1)
 
     @pl.when(mine == 0)
     def _():
@@ -272,7 +287,7 @@
     part[0:3] = jnp.zeros((3, 64, 128), F32)
     part[3] = jnp.ones((64, 128), F32)
 
-    def render_brick(j):
+    def sample_brick(j):
         for pair in range(4):
             both = jnp.concatenate(
                 [got[j, pl.ds(2 * pair + k, 64, stride=8), :] for k in range(2)], axis=1
@@ -288,29 +303,21 @@
                 second[at, 128:256] = low
         wide = dot_nt(second[...], col_rhs[...])
         samples[...] = wide[:, 0:128] + wide[:, 128:256]
+
+    def shade(j, at):
         coef = LOG2E * coefs[j]
-
-        @pl.loop(0, 2)
-        def _(block):
-            at = pl.multiple_of(block * 32, 32)
-            rows = pl.ds(at, 32)
-            opacity = jnp.where(entry_buf[rows, :] <= 8 * x + j, -STEP_LENGTH, 0.0)
-            red, green, blue, through = part[0, rows], part[1, rows], part[2, rows], part[3, rows]
-            for s in range(8):
-                value = samples[pl.ds(at + 64 * s, 32), :]
-                after = through * jnp.exp2(opacity * softplus2(coef[6:7] * value + coef[7:8]))
-                weight = through - after
-                through = after
-                red = red + weight * softplus2(coef[0:1] * value + coef[3:4])
-                green = green + weight * softplus2(coef[1:2] * value + coef[4:5])
-                blue = blue + weight * softplus2(coef[2:3] * value + coef[5:6])
-            part[0, rows], part[1, rows], part[2, rows], part[3, rows] = red, green, blue, through
-
-    for number, (first, count) in enumerate(ROUNDS):
-        with jax.named_scope("wait_brick"):
-            take(got.at[pl.ds(first, count), pl.ds(0, 480)], got_sem.at[number])
-        with jax.named_scope("bricks"):
-            pl.loop(first, first + count)(render_brick)
+        rows = pl.ds(at, 32)
+        opacity = jnp.where(entry_buf[rows, :] <= 8 * x + j, -STEP_LENGTH, 0.0)
+        red, green, blue, through = part[0, rows], part[1, rows], part[2, rows], part[3, rows]
+        for s in range(8):
+            value = samples[pl.ds(at + 64 * s, 32), :]
+            after = through * jnp.exp2(opacity * softplus2(coef[6:7] * value + coef[7:8]))
+            weight = through - after
+            through = after
+            red = red + weight * softplus2(coef[0:1] * value + coef[3:4])
+            green = green + weight * softplus2(coef[1:2] * value + coef[4:5])
+            blue = blue + weight * softplus2(coef[2:3] * value + coef[5:6])
+        part[0, rows], part[1, rows], part[2, rows], part[3, rows] = red, green, blue, through
 
     def final_copy(i):
         return remote(
@@ -318,8 +325,21 @@
             device(view_zh, view_core, zh, out_y, i),
         )
 
-    for i in range(4):
-        final_copy(i).start()
+    for number, (first, count) in enumerate(ROUNDS):
+        with jax.named_scope("wait_brick"):
+            take(got.at[pl.ds(first, count), pl.ds(0, 480)], got_sem.at[number])
+        with jax.named_scope("bricks"):
+            @pl.loop(first, first + count)
+            def _(j):
+                sample_brick(j)
+                if first + count < 8:
+                    pl.loop(0, 2)(lambda block: shade(j, pl.multiple_of(block * 32, 32)))
+                else:
+                    for block in range(2):
+                        shade(j, 32 * block)
+                        final_copy(2 * block).start()
+                        final_copy(2 * block + 1).start()
+
     with jax.named_scope("wait_finals"):
         take(finals, fin_got.at[0])
     total = finals[3, 0:3]
@@ -372,6 +392,7 @@
             pltpu.VMEM((4, 4, 16, 128), F32),
             dma((4, 4)), dma((3,)), dma((5,)), dma((5,)), dma((4,)), dma((4,)), dma((3,)), dma((3,)),
             dma((1,)), dma((1,)), dma((1,)), dma((1,)), dma((4,)), dma((1,)),
+            pltpu.SemaphoreType.REGULAR, pltpu.SemaphoreType.REGULAR,
         ],
         compiler_params=pltpu.CompilerParams(
             collective_id=0, has_side_effects=True, vmem_limit_bytes=60 * 1024 * 1024

time: 45.1 us -> 43.5 us (0.965)
  Pallas kernels: 44 us -> 42.8 us
    pallas_call x1, Pallas kernels: 44 us -> 42.8 us  [render(): pl.pallas_call(kernel, name='render', out_shape=pltpu.VMEM((1, 3, 16, 128...]
where the time goes in v3:
time: 43.5 us; the launch traced here: 43.4 us
  Pallas kernels  42.8 us (98%)
  local copies, waits for them, and re-layouts  0.61 us (1%)
    pallas_call x1, Pallas kernels, render(): pl.pallas_call(kernel, name='render', out_shape=pltpu.VMEM((1, 3, 16, 128...  42.8 us

profile of v3, /device:TPU:1, one launch (start us, length us, event | category | flops | bytes accessed | tf_op | source)
XLA Modules:
  0.0 43.4 jit_solution(5783807078661701273)
XLA Ops:
  0.0 42.8 %render.1 = f32[1,3,16,128]{3,2,1,0:T(8,128)S(1)} custom-call(f32[4,128,2048]{2,1,0:T(8,128)} %vol.1, f32[1,8,64]{2,1,0:T(8,128)} %step_map.1, f32[1,64,64]{2,1,0:T(8,128)} %rows_map.1, f32[1,64,64]{2,1,0:T(8,128)} %cols_map.1, f32[8,8]{1,0:T(8,128)} %table_in.1, s32[2,1,8]{2,1,0:T(1,128)} %bitcast.1, s32[1,512,128]{2,1,0:T(8,128)} %entry.1), custom_call_target="tpu_custom_call" | custom-call | tf_op jit(solution)/shard_map/render/pallas_call | solution.py:368
  42.8 0.6 %copy.9 = f32[1,3,16,128]{3,2,1,0:T(8,128)} copy(f32[1,3,16,128]{3,2,1,0:T(8,128)S(1)} %render.1) | data formatting | bytes 49152

commit v4 on v3

--- a/solution.py
+++ b/solution.py
@@ -52,7 +52,7 @@
     return jnp.concatenate([top, bottom], axis=0).astype(BF16)
 
 
-ROUNDS = ((0, 2), (2, 2), (4, 2), (6, 1), (7, 1))
+ROUNDS = ((0, 2), (2, 2), (4, 1), (5, 1), (6, 1), (7, 1))
 
 
 def kernel(
@@ -217,6 +217,9 @@
         (entry.at[0, pl.ds(to_rows, 64)], entry_buf),
     )
 
+    with jax.named_scope("relay"):
+        partner_copy.wait()
+        send_coefs(1 - zl, coef_relay)
     with jax.named_scope("wait_weights"):
         for copy in w_copies:
             copy.wait()
@@ -228,14 +231,10 @@
                 contract(lhs, rho, q, 1, 3)
                 if rho == 0:
                     send_round(0, (q,))
-        if rho == 0:
-            with jax.named_scope("relay"):
-                partner_copy.wait()
-                send_coefs(1 - zl, coef_relay)
         if rho > 0:
             with jax.named_scope("send_round"):
-                for number, (first, _) in enumerate(ROUNDS):
-                    if first // 2 == rho:
+                for number, (first, count) in enumerate(ROUNDS):
+                    if (first + count - 1) // 2 == rho:
                         send_round(number)
 
     pl.semaphore_wait(plane_ready, 1)
@@ -390,7 +389,7 @@
             pltpu.VMEM((512, 128), F32),
             pltpu.VMEM((4, 64, 128), F32),
             pltpu.VMEM((4, 4, 16, 128), F32),
-            dma((4, 4)), dma((3,)), dma((5,)), dma((5,)), dma((4,)), dma((4,)), dma((3,)), dma((3,)),
+            dma((4, 4)), dma((3,)), dma((len(ROUNDS),)), dma((len(ROUNDS),)), dma((4,)), dma((4,)), dma((3,)), dma((3,)),
             dma((1,)), dma((1,)), dma((1,)), dma((1,)), dma((4,)), dma((1,)),
             pltpu.SemaphoreType.REGULAR, pltpu.SemaphoreType.REGULAR,
         ],

time: 43.5 us -> 43.2 us (level)
  no operation moved by 1% of the time
where the time goes in v4:
time: 43.2 us; the launch traced here: 43.1 us
  Pallas kernels  42.5 us (98%)
  local copies, waits for them, and re-layouts  0.61 us (1%)
    pallas_call x1, Pallas kernels, render(): pl.pallas_call(kernel, name='render', out_shape=pltpu.VMEM((1, 3, 16, 128...  42.5 us

profile of v4, /device:TPU:1, one launch (start us, length us, event | category | flops | bytes accessed | tf_op | source)
XLA Modules:
  0.0 43.1 jit_solution(8268041551861097061)
XLA Ops:
  0.0 42.5 %render.1 = f32[1,3,16,128]{3,2,1,0:T(8,128)S(1)} custom-call(f32[4,128,2048]{2,1,0:T(8,128)} %vol.1, f32[1,8,64]{2,1,0:T(8,128)} %step_map.1, f32[1,64,64]{2,1,0:T(8,128)} %rows_map.1, f32[1,64,64]{2,1,0:T(8,128)} %cols_map.1, f32[8,8]{1,0:T(8,128)} %table_in.1, s32[2,1,8]{2,1,0:T(1,128)} %bitcast.1, s32[1,512,128]{2,1,0:T(8,128)} %entry.1), custom_call_target="tpu_custom_call" | custom-call | tf_op jit(solution)/shard_map/render/pallas_call | solution.py:367
  42.5 0.6 %copy.9 = f32[1,3,16,128]{3,2,1,0:T(8,128)} copy(f32[1,3,16,128]{3,2,1,0:T(8,128)S(1)} %render.1) | data formatting | bytes 49152

commit v5 on v4

--- a/solution.py
+++ b/solution.py
@@ -339,6 +339,17 @@
                         final_copy(2 * block).start()
                         final_copy(2 * block + 1).start()
 
+    with jax.named_scope("drain"):
+        for number in range(len(ROUNDS)):
+            sent_round(number)
+
+    @pl.when(mine != 0)
+    def _():
+        for i, (src, dst) in enumerate(maps):
+            remote(src, dst, map_send.at[i], map_got.at[i], to_device).wait_send()
+
+    coef_done(coef_send.at[0])
+
     with jax.named_scope("wait_finals"):
         take(finals, fin_got.at[0])
     total = finals[3, 0:3]
@@ -348,16 +359,6 @@
 
     for i in range(4):
         final_copy(i).wait_send()
-    with jax.named_scope("drain"):
-        for number in range(len(ROUNDS)):
-            sent_round(number)
-
-    @pl.when(mine != 0)
-    def _():
-        for i, (src, dst) in enumerate(maps):
-            remote(src, dst, map_send.at[i], map_got.at[i], to_device).wait_send()
-
-    coef_done(coef_send.at[0])
 
 
 def render(volume, step_weights, row_interp, col_interp, tf_table, materials, entry):

time: 43.2 us -> 43.2 us (level)
  no operation moved by 1% of the time
where the time goes in v5:
time: 43.2 us; the launch traced here: 43.1 us
  Pallas kernels  42.5 us (98%)
  local copies, waits for them, and re-layouts  0.61 us (1%)
    pallas_call x1, Pallas kernels, render(): pl.pallas_call(kernel, name='render', out_shape=pltpu.VMEM((1, 3, 16, 128...  42.5 us

profile of v5, /device:TPU:1, one launch (start us, length us, event | category | flops | bytes accessed | tf_op | source)
XLA Modules:
  0.0 43.1 jit_solution(3931598877166836851)
XLA Ops:
  0.0 42.5 %render.1 = f32[1,3,16,128]{3,2,1,0:T(8,128)S(1)} custom-call(f32[4,128,2048]{2,1,0:T(8,128)} %vol.1, f32[1,8,64]{2,1,0:T(8,128)} %step_map.1, f32[1,64,64]{2,1,0:T(8,128)} %rows_map.1, f32[1,64,64]{2,1,0:T(8,128)} %cols_map.1, f32[8,8]{1,0:T(8,128)} %table_in.1, s32[2,1,8]{2,1,0:T(1,128)} %bitcast.1, s32[1,512,128]{2,1,0:T(8,128)} %entry.1), custom_call_target="tpu_custom_call" | custom-call | tf_op jit(solution)/shard_map/render/pallas_call | solution.py:368
  42.5 0.6 %copy.9 = f32[1,3,16,128]{3,2,1,0:T(8,128)} copy(f32[1,3,16,128]{3,2,1,0:T(8,128)S(1)} %render.1) | data formatting | bytes 49152
